TPU v7x, 32 devices: a whole 2x2x4 slice. The times are simulated.
32 devices in a mesh: img: 4 (over y, core), txt: 8 (over z, x).
Axes of the slice: x: 2, y: 2, z: 4, core: 2. Of those that a mesh axis runs over, the one named last changes fastest.
Arguments:
- queries: bfloat16 [1, 5120, 8192], P(None, 'txt', 'img'), may hold values from -128 to 128
- visual_keys: bfloat16 [1, 512, 8192], P(None, 'img'), may hold values from -5 to 5
- visual_values: bfloat16 [1, 512, 8192], P(None, 'img'), may hold values from -6 to 6
- out_grad: bfloat16 [1, 5120, 8192], P(None, 'txt', 'img'), may hold values from -6 to 6
- gate_value: float32 [1, 64], P(None, 'img'), may hold values from -1.5 to 1.5
- image_order: int32 [1, 8], replicated, may hold values from 0 to 7, as said below
- image_seen: int32 [5120], P('txt'), may hold values from 1 to 8
Outputs:
- query_grad: bfloat16 [1, 5120, 8192], P(None, 'txt', 'img')
- key_grad: float32 [1, 512, 8192], P(None, 'txt', 'img')
- value_grad: float32 [1, 512, 8192], P(None, 'txt', 'img')
Inputs may be any that keep to these rules, and one draw needn't show every extreme that they name: `image_order`: each row names every image of 0 to 7 once.
All inputs are finite; a program needn't handle non-finite values.
Results may differ from a plain program's by a relative error of at most 0.0058.
Values may be sent and summed in bfloat16 or wider, within the bound.
A program may use at most 128 MiB of HBM per device.

v0:
```python
import math
import jax
import jax.numpy as jnp
from jax import lax
from jax.sharding import PartitionSpec as P


def image_mask(order_row, image_seen, key_count):
    image_count = order_row.shape[0]
    latent_count = key_count // image_count
    key_image = jnp.broadcast_to(order_row[:, None], (image_count, latent_count)).reshape(key_count)
    return key_image[None, :] < image_seen[:, None]


def attention_grads(query, grad_in, factor, key_rows, value_rows, allowed, score_scale):
    token_count = query.shape[0]
    head_count = factor.shape[0]
    head_width = query.shape[1] // head_count
    key_count = key_rows.shape[0]
    query_heads = query.reshape(token_count, head_count, head_width)
    key_heads = key_rows.reshape(key_count, head_count, head_width)
    value_heads = value_rows.reshape(key_count, head_count, head_width)
    gated_grad = (
        grad_in.reshape(token_count, head_count, head_width).astype(jnp.float32)
        * factor[None, :, None]
    ).astype(jnp.bfloat16)
    scores = (
        jnp.einsum("thd,khd->htk", query_heads, key_heads, preferred_element_type=jnp.float32)
        * score_scale
    )
    masked = jnp.where(allowed[None], scores, -1e30)
    row_max = jnp.max(masked, axis=2, keepdims=True)
    exponent = jnp.where(allowed[None], jnp.exp(masked - row_max), 0.0)
    weights = exponent / jnp.sum(exponent, axis=2, keepdims=True)
    weight_half = weights.astype(jnp.bfloat16)
    attended = jnp.einsum(
        "htk,khd->thd", weight_half, value_heads, preferred_element_type=jnp.float32
    )
    row_delta = jnp.sum(gated_grad.astype(jnp.float32) * attended, axis=2)
    weight_grad = jnp.einsum(
        "thd,khd->htk", gated_grad, value_heads, preferred_element_type=jnp.float32
    )
    score_half = (weights * (weight_grad - jnp.transpose(row_delta)[:, :, None])).astype(
        jnp.bfloat16
    )
    query_part = (
        jnp.einsum("htk,khd->thd", score_half, key_heads, preferred_element_type=jnp.float32)
        * score_scale
    )
    return (
        query_part.astype(jnp.bfloat16).reshape(token_count, -1),
        score_half,
        weight_half,
        query_heads,
        gated_grad,
    )


def latent_terms(score_half, weight_half, query_heads, gated_grad, count, score_scale):
    key_part = (
        jnp.einsum("htk,thd->khd", score_half, query_heads, preferred_element_type=jnp.float32)
        * score_scale
    )
    value_part = jnp.einsum(
        "htk,thd->khd", weight_half, gated_grad, preferred_element_type=jnp.float32
    )
    return (key_part.reshape(count, -1), value_part.reshape(count, -1))


def shards(queries, visual_keys, visual_values, out_grad, gate_value, image_order, image_seen):
    width_local = queries.shape[2]
    head_width = width_local // gate_value.shape[1]
    score_scale = 1.0 / math.sqrt(head_width)
    key_rows = lax.all_to_all(visual_keys[0], "img", split_axis=1, concat_axis=0, tiled=True)
    value_rows = lax.all_to_all(visual_values[0], "img", split_axis=1, concat_axis=0, tiled=True)
    key_total = key_rows.shape[0]
    allowed = image_mask(image_order[0], image_seen, key_total)
    factor = jnp.tanh(gate_value[0])
    query_part, score_half, weight_half, query_heads, gated_grad = attention_grads(
        queries[0], out_grad[0], factor, key_rows, value_rows, allowed, score_scale
    )
    query_list = [query_part]
    key_part, value_part = latent_terms(
        score_half, weight_half, query_heads, gated_grad, key_total, score_scale
    )
    key_share = lax.psum_scatter(key_part, "txt", scatter_dimension=0, tiled=True)
    value_share = lax.psum_scatter(value_part, "txt", scatter_dimension=0, tiled=True)
    key_list = [key_share]
    value_list = [value_share]
    key_grad = jnp.stack(key_list)
    value_grad = jnp.stack(value_list)
    return (jnp.stack(query_list), key_grad, value_grad)


def solution(mesh):
    placed = (
        P(None, "txt", "img"),
        P(None, "img", None),
        P(None, "img", None),
        P(None, "txt", "img"),
        P(None, "img"),
        P(),
        P("txt"),
    )
    return jax.shard_map(
        shards,
        mesh=mesh,
        in_specs=placed,
        out_specs=(P(None, "txt", "img"), P(None, "txt", "img"), P(None, "txt", "img")),
        check_vma=False,
    )
```

profile of v0, /device:TPU:0, one launch (start us, length us, event | category | flops | bytes accessed | tf_op | source)
XLA Modules:
  0.0 274.3 jit_solution(15759420821382776960)
XLA Ops:
  7.2 3.3 %all_to_all.24 = bf16[128,4,2048]{2,1,0:T(4,128)(2,1)S(1)} reshape(bf16[1,128,8192]{2,1,0:T(8,128)(2,1)} %param.8) | data formatting | bytes 4194304 | tf_op jit(solution)/shard_map/all_to_all | solution.py:74
  10.5 0.0 copy-start.4
  10.5 2.5 copy.24
  13.0 0.0 copy-start.2
  13.0 4.7 %all-to-all-start = ((bf16[128,4,2048]{2,0,1:T(8,128)(2,1)}), bf16[128,4,2048]{2,0,1:T(8,128)(2,1)}, u32[]{:S(2)}, u32[]{:S(2)}) async-start(bf16[128,4,2048]{2,0,1:T(8,128)(2,1)} %copy.24), calls=%async_computation | async-start | bytes 4194304 | tf_op jit(solution)/shard_map/all_to_all | solution.py:74
  17.8 0.0 reduce-scatter.5.cloned.1.call-start
  17.8 0.0 copy-done.4
  17.8 0.1 broadcast_in_dim.33
  17.9 0.1 lt.19
  18.0 0.0 copy-done.2
  18.0 2.6 copy.48
  20.5 0.0 copy-start.5
  20.5 0.0 copy-start.3
  20.5 4.9 %copy.27 = f32[1,640,2048]{1,2,0:T(8,128)} copy(bf16[1,640,2048]{2,1,0:T(8,128)(2,1)} %param.10) | data formatting | bytes 7864320 | tf_op jit(solution)/shard_map/convert_element_type | solution.py:24
  25.5 0.0 copy-done.5
  25.5 0.0 copy-done.3
  25.5 0.3 broadcast_compare_fusion
  25.7 3.1 %multiply_convert_fusion.2 = bf16[640,16,128]{0,2,1:T(8,128)(2,1)S(1)} fusion(f32[640,16,128]{0,2,1:T(8,128)} %bitcast.43, f32[16]{0:T(128)S(1)} %tanh_bitcast_fusion), kind=kLoop, calls=%fused_computation.13 | loop fusion | flops 2621440 | bytes 7864384 | tf_op jit(solution)/shard_map/convert_element_type | solution.py:26
  28.8 15.4 %all-to-all-done = bf16[128,4,2048]{2,0,1:T(8,128)(2,1)} async-done(((bf16[128,4,2048]{2,0,1:T(8,128)(2,1)}), bf16[128,4,2048]{2,0,1:T(8,128)(2,1)}, u32[]{:S(2)}, u32[]{:S(2)}) %all-to-all-start) | async-done | bytes 2097184 | tf_op jit(solution)/shard_map/all_to_all | solution.py:74
  44.2 3.6 %copy.49 = bf16[64,8,16,128]{3,2,1,0:T(8,128)(2,1)} copy(bf16[64,8,16,128]{3,1,2,0:T(8,128)(2,1)} %bitcast.20) | data formatting | bytes 4194304
  47.8 4.3 %copy.35 = bf16[512,16,128]{0,2,1:T(8,128)(2,1)} copy(bf16[512,16,128]{2,1,0:T(8,128)(2,1)} %bitcast.49) | data formatting | bytes 4194304 | tf_op jit(solution)/shard_map/reshape | solution.py:21
  52.1 14.4 %fusion.11 = (f32[16,640]{1,0:T(8,128)S(1)}, f32[16,640,512]{1,2,0:T(8,128)}) fusion(pred[640,512]{0,1:T(8,128)(4,1)S(1)} %broadcast_compare_fusion, bf16[640,16,128]{0,2,1:T(8,128)(2,1)} %bitcast.47, bf16[512,16,128]{0,2,1:T(8,128)(2,1)} %copy.35), kind=kOutput, calls=%fused_computation.20 | convolution fusion | flops 1368392192 | bytes 26058752 | tf_op jit(solution)/shard_map/sub | solution.py:33
  66.4 8.5 %fusion.5 = bf16[16,640,512]{1,2,0:T(8,128)(2,1)S(1)} fusion(f32[16,640,512]{1,2,0:T(8,128)} %get-tuple-element.10, f32[16,640]{1,0:T(8,128)S(1)} %get-tuple-element.9), kind=kLoop, calls=%fused_computation.9 | loop fusion | flops 10485760 | bytes 31498240 | tf_op jit(solution)/shard_map/convert_element_type | solution.py:35
  75.0 0.0 copy-start
  75.0 5.3 %fusion.12 = f32[16,128,512]{2,1,0:T(8,128)} fusion(bf16[640,16,128]{0,2,1:T(8,128)(2,1)S(1)} %multiply_convert_fusion.2, bf16[16,640,512]{1,2,0:T(8,128)(2,1)S(1)} %fusion.5), kind=kOutput, calls=%fused_computation.21 | convolution fusion | flops 1342177280 | bytes 17301504 | tf_op jit(solution)/shard_map/htk,thd->khd/dot_general | solution.py:64
  80.3 0.0 copy-done
  80.3 5.4 %copy.40 = f32[512,2048]{1,0:T(8,128)} copy(f32[512,2048]{0,1:T(8,128)} %bitcast.46) | data formatting | bytes 8388608 | tf_op jit(solution)/shard_map/reshape | solution.py:67
  85.7 0.0 reduce-scatter.5.cloned.1.call-update
  85.8 0.2 reduce-scatter.3.cloned.1.call-start
  86.0 4.5 %all_to_all.27 = bf16[128,4,2048]{2,1,0:T(4,128)(2,1)} reshape(bf16[1,128,8192]{2,1,0:T(8,128)(2,1)} %param.9) | data formatting | bytes 4194304 | tf_op jit(solution)/shard_map/all_to_all | solution.py:75
  90.5 2.7 %copy.28 = bf16[128,4,2048]{2,0,1:T(8,128)(2,1)S(1)} copy(bf16[128,4,2048]{2,1,0:T(4,128)(2,1)} %all_to_all.27) | data formatting | bytes 4194304 | tf_op jit(solution)/shard_map/all_to_all | solution.py:75
  93.3 28.1 %all_to_all.32 = bf16[128,4,2048]{2,0,1:T(8,128)(2,1)S(1)} all-to-all(bf16[128,4,2048]{2,0,1:T(8,128)(2,1)S(1)} %copy.28), channel_id=1, replica_groups=mesh['img'=4,'txt'=8] {'img'}, dimensions={1} | all-to-all | bytes 4194304 | tf_op jit(solution)/shard_map/all_to_all | solution.py:75
  121.4 1.9 copy.50
  123.3 4.3 %copy.32 = bf16[512,16,128]{0,2,1:T(8,128)(2,1)} copy(bf16[512,16,128]{2,1,0:T(8,128)(2,1)} %bitcast.51) | data formatting | bytes 4194304 | tf_op jit(solution)/shard_map/reshape | solution.py:22
  127.7 0.0 copy-start.1
  127.7 6.8 %fusion.6 = f32[640,16]{0,1:T(8,128)S(1)} fusion(bf16[640,16,128]{0,2,1:T(8,128)(2,1)S(1)} %multiply_convert_fusion.2, bf16[512,16,128]{0,2,1:T(8,128)(2,1)} %copy.32, bf16[16,640,512]{1,2,0:T(8,128)(2,1)} %copy-done), kind=kOutput, calls=%fused_computation.11 | convolution fusion | flops 1346099200 | bytes 15245312 | tf_op jit(solution)/shard_map/htk,khd->thd/dot_general | solution.py:36
  134.5 0.0 copy-done.1
  134.5 12.5 %multiply_convert_fusion = bf16[16,640,512]{1,2,0:T(8,128)(2,1)} fusion(f32[16,640]{1,0:T(8,128)S(1)} %bitcast.52, f32[16,640,512]{1,2,0:T(8,128)} %get-tuple-element.10, f32[16,640]{1,0:T(8,128)S(1)} %get-tuple-element.9, bf16[512,16,128]{0,2,1:T(8,128)(2,1)S(1)} %copy-done.1, bf16[640,16,128]{0,2,1:T(8,128)(2,1)S(1)} %multiply_convert_fusion.2), kind=kOutput, calls=%fused_computation.1 | convolution fusion | flops 1363148800 | bytes 36257792 | tf_op jit(solution)/shard_map/thd,khd->htk/dot_general | solution.py:40
  147.0 10.1 %broadcast_multiply_fusion = f32[16,512,128]{1,2,0:T(8,128)} fusion(bf16[16,640,512]{1,2,0:T(8,128)(2,1)} %multiply_convert_fusion, bf16[640,16,128]{0,2,1:T(8,128)(2,1)} %bitcast.48), kind=kOutput, calls=%fused_computation.14 | convolution fusion | flops 1343225856 | bytes 17301504 | tf_op jit(solution)/shard_map/htk,thd->khd/dot_general | solution.py:61
  157.0 5.4 %copy.38 = f32[512,2048]{1,0:T(8,128)} copy(f32[512,2048]{0,1:T(8,128)} %bitcast.45) | data formatting | bytes 8388608 | tf_op jit(solution)/shard_map/reshape | solution.py:67
  162.4 0.0 reduce-scatter.3.cloned.1.call-update
  162.5 6.6 %multiply_convert_fusion.1 = bf16[16,640,128]{1,2,0:T(8,128)(2,1)S(1)} fusion(bf16[512,16,128]{0,2,1:T(8,128)(2,1)} %copy.35, bf16[16,640,512]{1,2,0:T(8,128)(2,1)} %multiply_convert_fusion), kind=kOutput, calls=%fused_computation.12 | convolution fusion | flops 1344798720 | bytes 15204352 | tf_op jit(solution)/shard_map/htk,khd->thd/dot_general | solution.py:47
  169.1 2.6 copy.41
  171.7 3.6 %reduce-scatter.5.cloned.1.call-done = f32[64,2048]{1,0:T(8,128)} async-done(((f32[512,2048]{1,0:T(8,128)}), f32[64,2048]{1,0:T(8,128)}) %reduce-scatter.5.cloned.1.call-update) | async-done | bytes 524304 | tf_op jit(solution)/shard_map/reduce_scatter | solution.py:87
  175.3 92.2 %reduce-scatter.3.cloned.1.call-done = f32[64,2048]{1,0:T(8,128)} async-done(((f32[512,2048]{1,0:T(8,128)}), f32[64,2048]{1,0:T(8,128)}) %reduce-scatter.3.cloned.1.call-update) | async-done | bytes 524304 | tf_op jit(solution)/shard_map/reduce_scatter | solution.py:86
  (1 shorter events, 0.0 us)
Async XLA Ops:
  10.5 7.3 %copy-start.4 = (s32[1,8]{1,0:T(1,128)S(1)}, s32[1,8]{1,0:T(1,128)}, u32[]{:S(2)}) copy-start(s32[1,8]{1,0:T(1,128)} %param.12) | copy-start | bytes 100
  13.0 4.9 %copy-start.2 = (bf16[1,640,2048]{2,1,0:T(8,128)(2,1)S(1)}, bf16[1,640,2048]{2,1,0:T(8,128)(2,1)}, u32[]{:S(2)}) copy-start(bf16[1,640,2048]{2,1,0:T(8,128)(2,1)} %param.7) | copy-start | bytes 7864324
  13.0 31.2 %all-to-all-start = ((bf16[128,4,2048]{2,0,1:T(8,128)(2,1)}), bf16[128,4,2048]{2,0,1:T(8,128)(2,1)}, u32[]{:S(2)}, u32[]{:S(2)}) async-start(bf16[128,4,2048]{2,0,1:T(8,128)(2,1)} %copy.24), calls=%async_computation | async-start | bytes 4194304 | tf_op jit(solution)/shard_map/all_to_all | solution.py:74
  17.8 157.5 %reduce-scatter.5.cloned.1.call-start = ((), (), s32[]{:S(2)}) async-start(), calls=%async_computation.5 | async-start | bytes 4718592 | tf_op jit(solution)/shard_map/reduce_scatter | solution.py:87
  20.5 4.9 %copy-start.5 = (f32[1,16]{1,0:T(1,128)S(1)}, f32[1,16]{1,0:T(1,128)}, u32[]{:S(2)}) copy-start(f32[1,16]{1,0:T(1,128)} %param.11) | copy-start | bytes 196
  20.5 4.9 %copy-start.3 = (s32[640]{0:T(1024)S(1)}, s32[640]{0:T(1024)}, u32[]{:S(2)}) copy-start(s32[640]{0:T(1024)} %param.13) | copy-start | bytes 7684
  75.0 5.3 %copy-start = (bf16[16,640,512]{1,2,0:T(8,128)(2,1)}, bf16[16,640,512]{1,2,0:T(8,128)(2,1)S(1)}, u32[]{:S(2)}) copy-start(bf16[16,640,512]{1,2,0:T(8,128)(2,1)S(1)} %fusion.5) | copy-start | bytes 31457284
  85.8 181.7 %reduce-scatter.3.cloned.1.call-start = ((), (), s32[]{:S(2)}) async-start(), calls=%async_computation.4 | async-start | bytes 4718592 | tf_op jit(solution)/shard_map/reduce_scatter | solution.py:86
  127.7 6.8 %copy-start.1 = (bf16[512,16,128]{0,2,1:T(8,128)(2,1)S(1)}, bf16[512,16,128]{0,2,1:T(8,128)(2,1)}, u32[]{:S(2)}) copy-start(bf16[512,16,128]{0,2,1:T(8,128)(2,1)} %copy.32) | copy-start | bytes 6291460
Sparse Core Ops, SparseCore 0:
  85.9 89.3 reduce-scatter.4
  179.5 87.9 reduce-scatter.2
where the time goes:
time: 275 us; the launch traced here: 274 us
  waiting for transfers between devices  111 us (40%)
  matrix products  55.7 us (20%)
  local copies, waits for them, and re-layouts  48.4 us (18%)
  blocking collectives  28.1 us (10%)
  between operations  14.1 us (5%)
  other arithmetic  11.9 us (4%)
  starting transfers between devices  4.98 us (2%)
    reduce_scatter x1, waiting for transfers between devices, shards(): lax.psum_scatter(key_part, 'txt', scatter_dimension=0, tiled=True)  92.2 us
    all_to_all x1, blocking collectives, shards(): lax.all_to_all(visual_values[0], 'img', split_axis=1, concat_axis=0, tile...  28.1 us
    all_to_all x1, waiting for transfers between devices, shards(): lax.all_to_all(visual_keys[0], 'img', split_axis=1, concat_axis=0, tiled=...  15.4 us
    sub x1, matrix products, attention_grads(): exponent = jnp.where(allowed[None], jnp.exp(masked - row_max), 0.0)  14.4 us
    dot_general x1, matrix products, attention_grads(): jnp.einsum('thd,khd->htk', gated_grad, value_heads, preferred_element_typ...  12.5 us
    reshape x2, local copies, waits for them, and re-layouts, latent_terms(): return (key_part.reshape(count, -1), value_part.reshape(count, -1))  10.8 us
    dot_general x1, matrix products, latent_terms(): jnp.einsum('htk,thd->khd', score_half, query_heads, preferred_element_typ...  10.1 us
    convert_element_type x1, other arithmetic, attention_grads(): weight_half = weights.astype(jnp.bfloat16)  8.53 us
  transfers between devices with their start and end apart: 3, of which 3 were waited for; matrix products, arithmetic and copies ran while one was open for 23% of the time, Pallas kernels for 0%

commit v1 on v0

--- a/solution.py
+++ b/solution.py
@@ -71,7 +71,12 @@
     width_local = queries.shape[2]
     head_width = width_local // gate_value.shape[1]
     score_scale = 1.0 / math.sqrt(head_width)
-    key_rows = lax.all_to_all(visual_keys[0], "img", split_axis=1, concat_axis=0, tiled=True)
+    key_rows = jnp.concatenate(
+        lax.all_to_all(
+            jnp.stack(jnp.split(visual_keys[0], lax.axis_size("img"), axis=1)), "img", 0, 0
+        ),
+        axis=0,
+    )
     value_rows = lax.all_to_all(visual_values[0], "img", split_axis=1, concat_axis=0, tiled=True)
     key_total = key_rows.shape[0]
     allowed = image_mask(image_order[0], image_seen, key_total)

time: 275 us -> 272 us (0.989)
  local copies, waits for them, and re-layouts: 48.4 us -> 44.2 us
    another operation x0 -> x2, local copies, waits for them, and re-layouts: none -> 5.98 us  [the longest x1 4.32 us: attention_grads(): key_heads = key_rows.reshape(key_count, head_count, head_width)]
    all_to_all x2 -> x0, local copies, waits for them, and re-layouts: 5.85 us -> none  [shards(): lax.all_to_all(visual_keys[0], 'img', split_axis=1, concat_axis=0, tiled=...]
    reshape x1 -> x0, local copies, waits for them, and re-layouts: 4.31 us -> none  [attention_grads(): key_heads = key_rows.reshape(key_count, head_count, head_width)]
  transfers between devices with their start and end apart: 3 -> 3, of which waited for: 3 -> 3; matrix products, arithmetic and copies ran while one was open for 23% -> 24% of each run, Pallas kernels for 0% -> 0%
where the time goes in v1:
time: 272 us
  waiting for transfers between devices  111 us (41%)
  matrix products  55.6 us (20%)
  local copies, waits for them, and re-layouts  44.2 us (16%)
  blocking collectives  28.1 us (10%)
  between operations  14.1 us (5%)
  other arithmetic  13.5 us (5%)
  starting transfers between devices  4.54 us (2%)
    reduce_scatter x1, waiting for transfers between devices, shards(): lax.psum_scatter(key_part, 'txt', scatter_dimension=0, tiled=True)  92.2 us
    all_to_all x1, blocking collectives, shards(): lax.all_to_all(visual_values[0], 'img', split_axis=1, concat_axis=0, tile...  28.1 us
    all_to_all x1, waiting for transfers between devices, shards(): lax.all_to_all(jnp.stack(jnp.split(visual_keys[0], lax.axis_size('img'),...  15.4 us
    sub x1, matrix products, attention_grads(): exponent = jnp.where(allowed[None], jnp.exp(masked - row_max), 0.0)  14.4 us
    dot_general x1, matrix products, attention_grads(): jnp.einsum('thd,khd->htk', gated_grad, value_heads, preferred_element_typ...  12.4 us
    reshape x2, local copies, waits for them, and re-layouts, latent_terms(): return (key_part.reshape(count, -1), value_part.reshape(count, -1))  10.9 us
    dot_general x1, matrix products, latent_terms(): jnp.einsum('htk,thd->khd', score_half, query_heads, preferred_element_typ...  10.1 us
    convert_element_type x1, other arithmetic, attention_grads(): weight_half = weights.astype(jnp.bfloat16)  8.56 us
  transfers between devices with their start and end apart: 3, of which 3 were waited for; matrix products, arithmetic and copies ran while one was open for 24% of the time, Pallas kernels for 0%

profile of v1, /device:TPU:0, one launch (start us, length us, event | category | flops | bytes accessed | tf_op | source)
XLA Modules:
  0.0 271.5 jit_solution(15400720024568650520)
XLA Ops:
  7.2 1.7 slice_bitcast_fusion.3
  8.8 0.0 copy-start.4
  8.8 0.0 copy-start.2
  8.8 1.6 pad_maximum_fusion
  10.5 4.5 %all-to-all-start = ((bf16[4,128,2048]{2,1,0:T(8,128)(2,1)}), bf16[4,128,2048]{2,1,0:T(8,128)(2,1)}, u32[]{:S(2)}, u32[]{:S(2)}) async-start(bf16[4,128,2048]{2,1,0:T(8,128)(2,1)} %pad_maximum_fusion), calls=%async_computation | async-start | bytes 4194304 | tf_op jit(solution)/shard_map/all_to_all | solution.py:75
  15.0 0.0 reduce-scatter.5.cloned.1.call-start
  15.0 0.0 copy-done.4
  15.0 0.1 broadcast_in_dim.33
  15.1 0.1 lt.19
  15.2 0.0 copy-done.2
  15.2 2.6 copy.47
  17.7 0.0 copy-start.5
  17.7 0.0 copy-start.3
  17.7 4.9 %copy.26 = f32[1,640,2048]{1,2,0:T(8,128)} copy(bf16[1,640,2048]{2,1,0:T(8,128)(2,1)} %param.10) | data formatting | bytes 7864320 | tf_op jit(solution)/shard_map/convert_element_type | solution.py:24
  22.7 0.0 copy-done.5
  22.7 0.0 copy-done.3
  22.7 0.3 broadcast_compare_fusion
  22.9 3.1 %multiply_convert_fusion.2 = bf16[640,16,128]{0,2,1:T(8,128)(2,1)S(1)} fusion(f32[640,16,128]{0,2,1:T(8,128)} %bitcast.62, f32[16]{0:T(128)S(1)} %tanh_bitcast_fusion), kind=kLoop, calls=%fused_computation.13 | loop fusion | flops 2621440 | bytes 7864384 | tf_op jit(solution)/shard_map/convert_element_type | solution.py:26
  26.0 15.4 %all-to-all-done = bf16[4,128,2048]{2,1,0:T(8,128)(2,1)} async-done(((bf16[4,128,2048]{2,1,0:T(8,128)(2,1)}), bf16[4,128,2048]{2,1,0:T(8,128)(2,1)}, u32[]{:S(2)}, u32[]{:S(2)}) %all-to-all-start) | async-done | bytes 2097184 | tf_op jit(solution)/shard_map/all_to_all | solution.py:75
  41.4 3.6 %copy.48 = bf16[64,8,16,128]{3,2,1,0:T(8,128)(2,1)} copy(bf16[64,8,16,128]{3,1,2,0:T(8,128)(2,1)} %bitcast.25) | data formatting | bytes 4194304
  44.9 4.3 %copy.33 = bf16[512,16,128]{0,2,1:T(8,128)(2,1)} copy(bf16[512,16,128]{2,1,0:T(8,128)(2,1)} %bitcast.68) | data formatting | bytes 4194304 | tf_op jit(solution)/shard_map/reshape;reshape | solution.py:21
  49.3 14.4 %fusion.11 = (f32[16,640]{1,0:T(8,128)S(1)}, f32[16,640,512]{1,2,0:T(8,128)}) fusion(pred[640,512]{0,1:T(8,128)(4,1)S(1)} %broadcast_compare_fusion, bf16[512,16,128]{0,2,1:T(8,128)(2,1)} %copy.33, bf16[640,16,128]{0,2,1:T(8,128)(2,1)} %bitcast.66), kind=kOutput, calls=%fused_computation.25 | convolution fusion | flops 1368392192 | bytes 26058752 | tf_op jit(solution)/shard_map/sub | solution.py:33
  63.6 8.6 %fusion.5 = bf16[16,640,512]{1,2,0:T(8,128)(2,1)S(1)} fusion(f32[16,640,512]{1,2,0:T(8,128)} %get-tuple-element.14, f32[16,640]{1,0:T(8,128)S(1)} %get-tuple-element.13), kind=kLoop, calls=%fused_computation.9 | loop fusion | flops 10485760 | bytes 31498240 | tf_op jit(solution)/shard_map/convert_element_type | solution.py:35
  72.2 0.0 copy-start
  72.2 5.3 %fusion.12 = f32[16,128,512]{2,1,0:T(8,128)} fusion(bf16[640,16,128]{0,2,1:T(8,128)(2,1)S(1)} %multiply_convert_fusion.2, bf16[16,640,512]{1,2,0:T(8,128)(2,1)S(1)} %fusion.5), kind=kOutput, calls=%fused_computation.26 | convolution fusion | flops 1342177280 | bytes 17301504 | tf_op jit(solution)/shard_map/htk,thd->khd/dot_general | solution.py:64
  77.5 0.0 copy-done
  77.5 5.4 %copy.39 = f32[512,2048]{1,0:T(8,128)} copy(f32[512,2048]{0,1:T(8,128)} %bitcast.65) | data formatting | bytes 8388608 | tf_op jit(solution)/shard_map/reshape | solution.py:67
  82.9 0.0 reduce-scatter.5.cloned.1.call-update
  83.0 0.0 reduce-scatter.3.cloned.1.call-start
  83.0 4.5 %all_to_all.16 = bf16[128,4,2048]{2,1,0:T(4,128)(2,1)} reshape(bf16[1,128,8192]{2,1,0:T(8,128)(2,1)} %param.9) | data formatting | bytes 4194304 | tf_op jit(solution)/shard_map/all_to_all | solution.py:80
  87.5 2.7 %copy.27 = bf16[128,4,2048]{2,0,1:T(8,128)(2,1)S(1)} copy(bf16[128,4,2048]{2,1,0:T(4,128)(2,1)} %all_to_all.16) | data formatting | bytes 4194304 | tf_op jit(solution)/shard_map/all_to_all | solution.py:80
  90.3 28.1 %all_to_all.21 = bf16[128,4,2048]{2,0,1:T(8,128)(2,1)S(1)} all-to-all(bf16[128,4,2048]{2,0,1:T(8,128)(2,1)S(1)} %copy.27), channel_id=1, replica_groups=mesh['img'=4,'txt'=8] {'img'}, dimensions={1} | all-to-all | bytes 4194304 | tf_op jit(solution)/shard_map/all_to_all | solution.py:80
  118.4 1.9 copy.49
  120.4 4.3 %copy.31 = bf16[512,16,128]{0,2,1:T(8,128)(2,1)} copy(bf16[512,16,128]{2,1,0:T(8,128)(2,1)} %bitcast.70) | data formatting | bytes 4194304 | tf_op jit(solution)/shard_map/reshape | solution.py:22
  124.7 0.0 copy-start.1
  124.7 6.9 %fusion.6 = f32[640,16]{0,1:T(8,128)S(1)} fusion(bf16[640,16,128]{0,2,1:T(8,128)(2,1)S(1)} %multiply_convert_fusion.2, bf16[512,16,128]{0,2,1:T(8,128)(2,1)} %copy.31, bf16[16,640,512]{1,2,0:T(8,128)(2,1)} %copy-done), kind=kOutput, calls=%fused_computation.11 | convolution fusion | flops 1346099200 | bytes 15245312 | tf_op jit(solution)/shard_map/htk,khd->thd/dot_general | solution.py:36
  131.5 0.0 copy-done.1
  131.5 12.4 %multiply_convert_fusion = bf16[16,640,512]{1,2,0:T(8,128)(2,1)} fusion(f32[16,640]{1,0:T(8,128)S(1)} %bitcast.72, f32[16,640,512]{1,2,0:T(8,128)} %get-tuple-element.14, f32[16,640]{1,0:T(8,128)S(1)} %get-tuple-element.13, bf16[512,16,128]{0,2,1:T(8,128)(2,1)S(1)} %copy-done.1, bf16[640,16,128]{0,2,1:T(8,128)(2,1)S(1)} %multiply_convert_fusion.2), kind=kOutput, calls=%fused_computation.2 | convolution fusion | flops 1363148800 | bytes 36257792 | tf_op jit(solution)/shard_map/thd,khd->htk/dot_general | solution.py:40
  144.0 10.1 %broadcast_multiply_fusion = f32[16,512,128]{1,2,0:T(8,128)} fusion(bf16[16,640,512]{1,2,0:T(8,128)(2,1)} %multiply_convert_fusion, bf16[640,16,128]{0,2,1:T(8,128)(2,1)} %bitcast.67), kind=kOutput, calls=%fused_computation.15 | convolution fusion | flops 1343225856 | bytes 17301504 | tf_op jit(solution)/shard_map/htk,thd->khd/dot_general | solution.py:61
  154.1 5.5 %copy.37 = f32[512,2048]{1,0:T(8,128)} copy(f32[512,2048]{0,1:T(8,128)} %bitcast.64) | data formatting | bytes 8388608 | tf_op jit(solution)/shard_map/reshape | solution.py:67
  159.5 0.0 reduce-scatter.3.cloned.1.call-update
  159.5 6.6 %multiply_convert_fusion.1 = bf16[16,128,640]{2,1,0:T(8,128)(2,1)S(1)} fusion(bf16[512,16,128]{0,2,1:T(8,128)(2,1)} %copy.33, bf16[16,640,512]{1,2,0:T(8,128)(2,1)} %multiply_convert_fusion), kind=kOutput, calls=%fused_computation.12 | convolution fusion | flops 1344798720 | bytes 15204352 | tf_op jit(solution)/shard_map/htk,khd->thd/dot_general | solution.py:47
  166.1 2.6 copy.40
  168.7 3.7 %reduce-scatter.5.cloned.1.call-done = f32[64,2048]{1,0:T(8,128)} async-done(((f32[512,2048]{1,0:T(8,128)}), f32[64,2048]{1,0:T(8,128)}) %reduce-scatter.5.cloned.1.call-update) | async-done | bytes 524304 | tf_op jit(solution)/shard_map/reduce_scatter | solution.py:92
  172.5 92.2 %reduce-scatter.3.cloned.1.call-done = f32[64,2048]{1,0:T(8,128)} async-done(((f32[512,2048]{1,0:T(8,128)}), f32[64,2048]{1,0:T(8,128)}) %reduce-scatter.3.cloned.1.call-update) | async-done | bytes 524304 | tf_op jit(solution)/shard_map/reduce_scatter | solution.py:91
  (1 shorter events, 0.0 us)
Async XLA Ops:
  8.8 6.2 %copy-start.4 = (s32[1,8]{1,0:T(1,128)S(1)}, s32[1,8]{1,0:T(1,128)}, u32[]{:S(2)}) copy-start(s32[1,8]{1,0:T(1,128)} %param.12) | copy-start | bytes 100
  8.8 6.3 %copy-start.2 = (bf16[1,640,2048]{2,1,0:T(8,128)(2,1)S(1)}, bf16[1,640,2048]{2,1,0:T(8,128)(2,1)}, u32[]{:S(2)}) copy-start(bf16[1,640,2048]{2,1,0:T(8,128)(2,1)} %param.7) | copy-start | bytes 7864324
  10.5 30.9 %all-to-all-start = ((bf16[4,128,2048]{2,1,0:T(8,128)(2,1)}), bf16[4,128,2048]{2,1,0:T(8,128)(2,1)}, u32[]{:S(2)}, u32[]{:S(2)}) async-start(bf16[4,128,2048]{2,1,0:T(8,128)(2,1)} %pad_maximum_fusion), calls=%async_computation | async-start | bytes 4194304 | tf_op jit(solution)/shard_map/all_to_all | solution.py:75
  15.0 157.5 %reduce-scatter.5.cloned.1.call-start = ((), (), s32[]{:S(2)}) async-start(), calls=%async_computation.5 | async-start | bytes 4718592 | tf_op jit(solution)/shard_map/reduce_scatter | solution.py:92
  17.7 4.9 %copy-start.5 = (f32[1,16]{1,0:T(1,128)S(1)}, f32[1,16]{1,0:T(1,128)}, u32[]{:S(2)}) copy-start(f32[1,16]{1,0:T(1,128)} %param.11) | copy-start | bytes 196
  17.7 4.9 %copy-start.3 = (s32[640]{0:T(1024)S(1)}, s32[640]{0:T(1024)}, u32[]{:S(2)}) copy-start(s32[640]{0:T(1024)} %param.13) | copy-start | bytes 7684
  72.2 5.3 %copy-start = (bf16[16,640,512]{1,2,0:T(8,128)(2,1)}, bf16[16,640,512]{1,2,0:T(8,128)(2,1)S(1)}, u32[]{:S(2)}) copy-start(bf16[16,640,512]{1,2,0:T(8,128)(2,1)S(1)} %fusion.5) | copy-start | bytes 31457284
  83.0 181.7 %reduce-scatter.3.cloned.1.call-start = ((), (), s32[]{:S(2)}) async-start(), calls=%async_computation.4 | async-start | bytes 4718592 | tf_op jit(solution)/shard_map/reduce_scatter | solution.py:91
  124.7 6.9 %copy-start.1 = (bf16[512,16,128]{0,2,1:T(8,128)(2,1)S(1)}, bf16[512,16,128]{0,2,1:T(8,128)(2,1)}, u32[]{:S(2)}) copy-start(bf16[512,16,128]{0,2,1:T(8,128)(2,1)} %copy.31) | copy-start | bytes 6291460
Sparse Core Ops, SparseCore 0:
  83.1 89.3 reduce-scatter.4
  176.7 87.9 reduce-scatter.2
